TPU v7x, 32 devices: a whole 2x2x4 slice. The times are simulated.
32 devices in a mesh: subset: 8 (over z, x), vocab: 4 (over y, core).
Axes of the slice: x: 2, y: 2, z: 4, core: 2. Of those that a mesh axis runs over, the one named last changes fastest.
Arguments:
- hidden: bfloat16 [4096, 2048], P('subset', 'vocab'), may hold values from -100 to 100
- proj_weight: bfloat16 [2048, 25600], P('subset', 'vocab'), may hold values from -1 to 1
- targets: int32 [4096], P('subset'), may hold values from 0 to 25599
- counts: int32 [8, 100, 512], P('subset', 'vocab'), may hold values from 1 to 15, as said below
- ranks: int32 [8], replicated, may hold values from 0 to 799
Outputs:
- row_cross_entropy: float32 [4096], P('subset')
- resample_mean_losses: float32 [8, 100], P('subset', 'vocab')
- quantiles: float32 [8], replicated
Inputs may be any that keep to these rules, and one draw needn't show every extreme that they name: For every subset and resample the counts over the 512 rows sum to 4096.
All inputs are finite; a program needn't handle non-finite values.
Results may differ from a plain program's by a relative error of at most 0.0003.
Values may be sent and summed in bfloat16 or wider, within the bound.
No kernel may reach another device: no remote copies, remote signals or barrier semaphores. Data moves between devices by JAX's collectives and lax.ppermute only.
A program may use at most 128 MiB of HBM per device.

v0:
```python
import jax
import jax.numpy as jnp
from jax import lax
from jax.sharding import PartitionSpec as P


def shards(hidden, proj_weight, targets, counts, ranks):
    features = lax.all_gather(hidden, "vocab", axis=1, tiled=True)
    columns = proj_weight.shape[1]
    whole_weight = lax.all_gather(proj_weight, "subset", axis=0, tiled=True)
    logit_scores = jnp.dot(features, whole_weight, preferred_element_type=jnp.float32)
    local_top = jnp.max(logit_scores, axis=1)
    local_sum = jnp.sum(jnp.exp(logit_scores - local_top[:, None]), axis=1)
    offset = targets - lax.axis_index("vocab") * columns
    inside = (offset >= 0) & (offset < columns)
    picked = jnp.take_along_axis(logit_scores, jnp.clip(offset, 0, columns - 1)[:, None], axis=1)[
        :, 0
    ]
    picked = jnp.where(inside, picked, 0.0)
    row_max = lax.pmax(local_top, "vocab")
    row_total, target_logit = lax.psum((local_sum * jnp.exp(local_top - row_max), picked), "vocab")
    row_cross_entropy = row_max + jnp.log(row_total) - target_logit
    total_rows = 1.0 * lax.axis_size("subset") * row_cross_entropy.shape[0]
    resample_mean_losses = (
        jnp.einsum(
            "cno,o->cn",
            counts.astype(jnp.float32),
            row_cross_entropy,
            precision=lax.Precision.HIGHEST,
        )
        / total_rows
    )
    grouped = lax.all_gather(resample_mean_losses, "vocab", axis=1, tiled=True)
    gathered = lax.all_gather(grouped, "subset", axis=0, tiled=True)
    pooled = jnp.sort(gathered.reshape(-1))
    positions = lax.iota(jnp.int32, pooled.shape[0])
    chosen = positions[:, None] == ranks[None, :]
    quantiles = jnp.sum(jnp.where(chosen, pooled[:, None], 0.0), axis=0)
    return (row_cross_entropy, resample_mean_losses, quantiles)


def solution(mesh):
    return jax.shard_map(
        shards,
        mesh=mesh,
        in_specs=(
            P("subset", "vocab"),
            P("subset", "vocab"),
            P("subset"),
            P("subset", "vocab", None),
            P(),
        ),
        out_specs=(P("subset"), P("subset", "vocab"), P()),
        check_vma=False,
    )
```

profile of v0, /device:TPU:0, one launch (start us, length us, event | category | flops | bytes accessed | tf_op | source)
XLA Modules:
  0.0 625.1 jit_solution(13795552494358012324)
XLA Ops:
  7.2 0.0 all-gather.5.cloned.1.call-start
  7.2 0.7 all-gather.5.cloned.1.call-update
  7.9 0.0 all-gather.7.cloned.1.call-start
  7.9 0.7 all-gather.7.cloned.1.call-update
  8.7 0.8 convert_element_type.3
  9.5 1.2 dynamic-slice
  10.8 1.2 dynamic-slice.1
  13.3 0.7 compare_select_fusion
  14.0 20.8 %all-gather.5.cloned.1.call-done = bf16[512,2048]{1,0:T(8,128)(2,1)} async-done(((bf16[512,512]{1,0:T(8,128)(2,1)}), bf16[512,2048]{1,0:T(8,128)(2,1)}) %all-gather.5.cloned.1.call-update) | async-done | bytes 2097168 | tf_op jit(solution)/shard_map/all_gather | solution.py:8
  34.9 501.6 %all-gather.7.cloned.1.call-done = bf16[2048,6400]{1,0:T(8,128)(2,1)} async-done(((bf16[256,6400]{1,0:T(8,128)(2,1)}), bf16[2048,6400]{1,0:T(8,128)(2,1)}) %all-gather.7.cloned.1.call-update) | async-done | bytes 26214416 | tf_op jit(solution)/shard_map/all_gather | solution.py:10
  536.4 22.5 %fusion.6 = (f32[512]{0:T(512)S(1)}, f32[512,6400]{1,0:T(8,128)}) fusion(bf16[512,2048]{1,0:T(8,128)(2,1)} %all-gather.5.cloned.1.call-done, bf16[2048,6400]{1,0:T(8,128)(2,1)} %all-gather.7.cloned.1.call-done), kind=kOutput, calls=%fused_computation.18 | convolution fusion | flops 13425049600 | bytes 41420800 | tf_op jit(solution)/shard_map/dot_general | solution.py:11
  558.9 6.5 %pmax.7 = f32[512]{0:T(512)S(1)} all-reduce(f32[512]{0:T(512)S(1)} %get-tuple-element.8), channel_id=1, replica_groups=mesh['subset'=8,'vocab'=4] {'vocab'}, use_global_device_ids=true, to_apply=%region_1.0 | all-reduce | flops 512 | bytes 4096 | tf_op jit(solution)/shard_map/pmax | solution.py:20
  565.5 6.6 %exponential_reduce_fusion = f32[512]{0:T(512)S(1)} fusion(f32[512,6400]{1,0:T(8,128)} %get-tuple-element.9, f32[512]{0:T(512)S(1)} %get-tuple-element.8), kind=kLoop, calls=%fused_computation.1 | loop fusion | flops 6553088 | bytes 13111296 | tf_op jit(solution)/shard_map/reduce_sum | solution.py:13
  572.0 8.2 %gather_fusion = f32[512]{0:T(512)S(1)} fusion(f32[512,6400]{1,0:T(8,128)} %get-tuple-element.9, s32[512]{0:T(512)S(1)} %bitcast.18), kind=kCustom, calls=%fused_computation | custom fusion | bytes 8192 | tf_op jit(solution)/shard_map/jit(take_along_axis)/gather | solution.py:16
  580.2 0.0 copy-done
  580.2 5.8 all-reduce.2
  586.1 0.1 fusion
  586.3 0.2 dynamic-update-slice
  586.5 5.7 all-reduce
  592.3 0.2 dynamic-update-slice.1
  592.5 20.5 %all-reduce.1 = f32[800]{0:T(1024)S(1)} all-reduce(f32[800]{0:T(1024)S(1)} %dynamic-update-slice.1), channel_id=3, replica_groups=mesh['subset'=8,'vocab'=4] {'subset'}, use_global_device_ids=true, to_apply=%add.1 | all-reduce | flops 800 | bytes 6400
  613.0 4.5 sort.15
  617.6 0.7 select_reduce_fusion
  618.3 0.0 copy-done.1
  (15 shorter events, 0.1 us)
Async XLA Ops:
  7.2 27.7 %all-gather.5.cloned.1.call-start = ((), (), s32[]{:S(2)}) async-start(), calls=%async_computation | async-start | bytes 2621440 | tf_op jit(solution)/shard_map/all_gather | solution.py:8
  7.9 528.6 %all-gather.7.cloned.1.call-start = ((), (), s32[]{:S(2)}) async-start(), calls=%async_computation.1 | async-start | bytes 29491200 | tf_op jit(solution)/shard_map/all_gather | solution.py:10
  558.9 21.3 %copy-start = (s32[512]{0:T(512)S(1)}, s32[512]{0:T(512)}, u32[]{:S(2)}) copy-start(s32[512]{0:T(512)} %param.7) | copy-start | bytes 6148
  558.9 58.6 %copy-start.3 = (s32[8]{0:T(128)S(1)}, s32[8]{0:T(128)}, u32[]{:S(2)}) copy-start(s32[8]{0:T(128)} %param.9) | copy-start | bytes 100
  586.1 32.2 %copy-start.1 = (f32[512]{0:T(512)}, f32[512]{0:T(512)S(1)}, u32[]{:S(2)}) copy-start(f32[512]{0:T(512)S(1)} %add_subtract_fusion) | copy-start | bytes 6148
  586.2 32.0 %copy-start.2 = (f32[25]{0:T(128)}, f32[25]{0:T(128)S(1)}, u32[]{:S(2)}) copy-start(f32[25]{0:T(128)S(1)} %fusion) | copy-start | bytes 304
Sparse Core Ops, SparseCore 0:
  9.5 25.2 all-gather.4
  36.4 500.0 all-gather.6
where the time goes:
time: 626 us; the launch traced here: 625 us
  waiting for transfers between devices  524 us (84%)
  blocking collectives  38.6 us (6%)
  matrix products  22.6 us (4%)
  between operations  15.4 us (2%)
  other arithmetic  13.4 us (2%)
  local copies, waits for them, and re-layouts  11.1 us (2%)
    all_gather x1, waiting for transfers between devices, shards(): whole_weight = lax.all_gather(proj_weight, 'subset', axis=0, tiled=True)  502 us
    unnamed x2, blocking collectives  26.3 us
    dot_general x1, matrix products, shards(): jnp.dot(features, whole_weight, preferred_element_type=jnp.float32)  22.5 us
    all_gather x1, waiting for transfers between devices, shards(): features = lax.all_gather(hidden, 'vocab', axis=1, tiled=True)  20.8 us
  transfers between devices with their start and end apart: 2, of which 2 were waited for; matrix products, arithmetic and copies ran while one was open for 1% of the time, Pallas kernels for 0%

commit v1 on v0

--- a/solution.py
+++ b/solution.py
@@ -2,12 +2,27 @@
 import jax.numpy as jnp
 from jax import lax
 from jax.sharding import PartitionSpec as P
+from jax.lax import axis_index, axis_size, ppermute
 
 
 def shards(hidden, proj_weight, targets, counts, ranks):
     features = lax.all_gather(hidden, "vocab", axis=1, tiled=True)
     columns = proj_weight.shape[1]
-    whole_weight = lax.all_gather(proj_weight, "subset", axis=0, tiled=True)
+
+    def extend_roots_in(tile_in, net_axis):
+        world_n = axis_size(net_axis)
+        sides = [tile_in]
+        for pp in [*range(world_n - 1)]:
+            sides.append(
+                ppermute(sides[-1], net_axis, [(jj, (jj + 1) % world_n) for jj in range(world_n)])
+            )
+        return jnp.roll(
+            jnp.concatenate(sides[::-1], axis=0),
+            (axis_index(net_axis) + 1) * tile_in.shape[0],
+            axis=0,
+        )
+
+    whole_weight = extend_roots_in(proj_weight, "subset")
     logit_scores = jnp.dot(features, whole_weight, preferred_element_type=jnp.float32)
     local_top = jnp.max(logit_scores, axis=1)
     local_sum = jnp.sum(jnp.exp(logit_scores - local_top[:, None]), axis=1)

time: 626 us -> 675 us (1.078)
  local copies, waits for them, and re-layouts: 11.1 us -> 80 us
  waiting for transfers between devices: 524 us -> 504 us
    ppermute x0 -> x7, waiting for transfers between devices: none -> 504 us  [extend_roots_in(): ppermute(sides[-1], net_axis, [(jj, (jj + 1) % world_n) for jj in range(w...]
    all_gather x1 -> x0, waiting for transfers between devices: 502 us -> none  [shards(): whole_weight = lax.all_gather(proj_weight, 'subset', axis=0, tiled=True)]
    unnamed x15 -> x52, local copies, waits for them, and re-layouts: 2.99 us -> 59.5 us
    all_gather x1, waiting for transfers between devices: 20.8 us -> 0.01 us  [shards(): features = lax.all_gather(hidden, 'vocab', axis=1, tiled=True)]
    gather x1, local copies, waits for them, and re-layouts: 8.15 us -> 18.6 us  [shards(): jnp.take_along_axis(logit_scores, jnp.clip(offset, 0, columns - 1)[:, Non...]
  transfers between devices with their start and end apart: 2 -> 8, of which waited for: 2 -> 7; matrix products, arithmetic and copies ran while one was open for 1% -> 8% of each run, Pallas kernels for 0% -> 0%
where the time goes in v1:
time: 675 us; the launch traced here: 674 us
  waiting for transfers between devices  504 us (75%)
  local copies, waits for them, and re-layouts  80 us (12%)
  blocking collectives  34.5 us (5%)
  matrix products  22.5 us (3%)
  between operations  16 us (2%)
  other arithmetic  14.2 us (2%)
    ppermute x7, waiting for transfers between devices, extend_roots_in(): ppermute(sides[-1], net_axis, [(jj, (jj + 1) % world_n) for jj in range(w...  504 us
    unnamed x52, local copies, waits for them, and re-layouts  59.5 us
    unnamed x2, blocking collectives  22.9 us
    dot_general x1, matrix products, shards(): jnp.dot(features, whole_weight, preferred_element_type=jnp.float32)  22.4 us
    gather x1, local copies, waits for them, and re-layouts, shards(): jnp.take_along_axis(logit_scores, jnp.clip(offset, 0, columns - 1)[:, Non...  18.6 us
  transfers between devices with their start and end apart: 8, of which 7 were waited for; matrix products, arithmetic and copies ran while one was open for 8% of the time, Pallas kernels for 0%

profile of v1, /device:TPU:0, one launch (start us, length us, event | category | flops | bytes accessed | tf_op | source)
XLA Modules:
  0.0 673.8 jit_solution(649817708830700547)
XLA Ops:
  10.2 74.2 %collective-permute-done = bf16[256,6400]{1,0:T(8,128)(2,1)S(1)} collective-permute-done((bf16[256,6400]{1,0:T(8,128)(2,1)}, bf16[256,6400]{1,0:T(8,128)(2,1)S(1)}, u32[]{:S(2)}, u32[]{:S(2)}) %collective-permute-start) | collective-permute-done | bytes 3276832 | tf_op jit(solution)/shard_map/ppermute | solution.py:17
  86.1 74.8 %collective-permute-done.1 = bf16[256,6400]{1,0:T(8,128)(2,1)S(1)} collective-permute-done((bf16[256,6400]{1,0:T(8,128)(2,1)S(1)}, bf16[256,6400]{1,0:T(8,128)(2,1)S(1)}, u32[]{:S(2)}, u32[]{:S(2)}) %collective-permute-start.1) | collective-permute-done | bytes 3276832 | tf_op jit(solution)/shard_map/ppermute | solution.py:17
  162.6 73.9 %collective-permute-done.2 = bf16[256,6400]{1,0:T(8,128)(2,1)S(1)} collective-permute-done((bf16[256,6400]{1,0:T(8,128)(2,1)S(1)}, bf16[256,6400]{1,0:T(8,128)(2,1)S(1)}, u32[]{:S(2)}, u32[]{:S(2)}) %collective-permute-start.2) | collective-permute-done | bytes 3276832 | tf_op jit(solution)/shard_map/ppermute | solution.py:17
  238.2 73.1 %collective-permute-done.3 = bf16[256,6400]{1,0:T(8,128)(2,1)S(1)} collective-permute-done((bf16[256,6400]{1,0:T(8,128)(2,1)S(1)}, bf16[256,6400]{1,0:T(8,128)(2,1)S(1)}, u32[]{:S(2)}, u32[]{:S(2)}) %collective-permute-start.3) | collective-permute-done | bytes 3276832 | tf_op jit(solution)/shard_map/ppermute | solution.py:17
  313.0 72.2 %collective-permute-done.4 = bf16[256,6400]{1,0:T(8,128)(2,1)S(1)} collective-permute-done((bf16[256,6400]{1,0:T(8,128)(2,1)S(1)}, bf16[256,6400]{1,0:T(8,128)(2,1)S(1)}, u32[]{:S(2)}, u32[]{:S(2)}) %collective-permute-start.4) | collective-permute-done | bytes 3276832 | tf_op jit(solution)/shard_map/ppermute | solution.py:17
  386.9 71.4 %collective-permute-done.5 = bf16[256,6400]{1,0:T(8,128)(2,1)} collective-permute-done((bf16[256,6400]{1,0:T(8,128)(2,1)S(1)}, bf16[256,6400]{1,0:T(8,128)(2,1)}, u32[]{:S(2)}, u32[]{:S(2)}) %collective-permute-start.5) | collective-permute-done | bytes 3276832 | tf_op jit(solution)/shard_map/ppermute | solution.py:17
  465.2 64.0 %collective-permute-done.6 = bf16[256,6400]{1,0:T(8,128)(2,1)} collective-permute-done((bf16[256,6400]{1,0:T(8,128)(2,1)}, bf16[256,6400]{1,0:T(8,128)(2,1)}, u32[]{:S(2)}, u32[]{:S(2)}) %collective-permute-start.6) | collective-permute-done | bytes 3276832 | tf_op jit(solution)/shard_map/ppermute | solution.py:17
  529.2 3.8 constant_dynamic-update-slice_fusion.15
  533.0 3.9 constant_dynamic-update-slice_fusion.14
  536.8 3.9 constant_dynamic-update-slice_fusion.13
  540.7 3.9 constant_dynamic-update-slice_fusion.12
  548.4 3.8 constant_dynamic-update-slice_fusion.10
  552.2 3.9 constant_dynamic-update-slice_fusion.9
  556.1 3.9 constant_dynamic-update-slice_fusion.8
  560.0 3.8 constant_dynamic-update-slice_fusion.7
  563.8 3.8 constant_dynamic-update-slice_fusion.6
  579.0 22.4 %fusion.9 = (f32[512]{0:T(512)S(1)}, f32[6400,512]{1,0:T(8,128)}) fusion(bf16[512,2048]{1,0:T(8,128)(2,1)} %all-gather.4.cloned.1.call-done, bf16[4096,6400]{1,0:T(8,128)(2,1)} %constant_dynamic-update-slice_fusion, s32[]{:T(128)S(6)} %select_n.50), kind=kOutput, calls=%fused_computation.37 | convolution fusion | flops 13425049600 | bytes 41420804 | tf_op jit(solution)/shard_map/dot_general | solution.py:26
  601.4 5.9 pmax.7
  607.3 6.5 exponential_reduce_fusion
  613.8 18.6 %gather_fusion = f32[512]{0:T(512)S(1)} fusion(f32[512,6400]{0,1:T(8,128)} %bitcast.20, s32[512]{0:T(512)S(1)} %bitcast.19), kind=kCustom, calls=%fused_computation | custom fusion | bytes 8192 | tf_op jit(solution)/shard_map/jit(take_along_axis)/gather | solution.py:31
  632.4 5.8 all-reduce.2
  638.6 5.7 all-reduce
  644.6 17.1 %all-reduce.1 = f32[800]{0:T(1024)S(1)} all-reduce(f32[800]{0:T(1024)S(1)} %dynamic-update-slice.1), channel_id=3, replica_groups=mesh['subset'=8,'vocab'=4] {'subset'}, use_global_device_ids=true, to_apply=%add.1 | all-reduce | flops 800 | bytes 6400
  661.7 4.5 sort.15
  (64 shorter events, 33.1 us)
Async XLA Ops:
  7.2 570.0 %copy-start = (bf16[256,6400]{1,0:T(8,128)(2,1)S(1)}, bf16[256,6400]{1,0:T(8,128)(2,1)}, u32[]{:S(2)}) copy-start(bf16[256,6400]{1,0:T(8,128)(2,1)} %param.6) | copy-start | bytes 9830404
  7.2 571.9 %all-gather.4.cloned.1.call-start = ((), (), s32[]{:S(2)}) async-start(), calls=%async_computation | async-start | bytes 2621440 | tf_op jit(solution)/shard_map/all_gather | solution.py:9
  7.2 77.2 %collective-permute-start = (bf16[256,6400]{1,0:T(8,128)(2,1)}, bf16[256,6400]{1,0:T(8,128)(2,1)S(1)}, u32[]{:S(2)}, u32[]{:S(2)}) collective-permute-start(bf16[256,6400]{1,0:T(8,128)(2,1)} %param.6), channel_id=1, source_target_pairs={{0,4},{4,8},{8,12},{12,16},{16,20},{20,24},{24,28},{28,0},{1,5},{5... | collective-permute-start | bytes 9830408 | tf_op jit(solution)/shard_map/ppermute | solution.py:17
  84.4 1.7 copy-start.1
  86.1 74.8 %collective-permute-start.1 = (bf16[256,6400]{1,0:T(8,128)(2,1)S(1)}, bf16[256,6400]{1,0:T(8,128)(2,1)S(1)}, u32[]{:S(2)}, u32[]{:S(2)}) collective-permute-start(bf16[256,6400]{1,0:T(8,128)(2,1)S(1)} %collective-permute-done), channel_id=1, source_target_pairs={{0,4},{4,8},{8,12},{12,16},{16,20},{20,24},{24,28},{28,0},{1,5},{5... | collective-permute-start | bytes 9830408 | tf_op jit(solution)/shard_map/ppermute | solution.py:17
  160.9 1.7 copy-start.3
  162.6 73.9 %collective-permute-start.2 = (bf16[256,6400]{1,0:T(8,128)(2,1)S(1)}, bf16[256,6400]{1,0:T(8,128)(2,1)S(1)}, u32[]{:S(2)}, u32[]{:S(2)}) collective-permute-start(bf16[256,6400]{1,0:T(8,128)(2,1)S(1)} %collective-permute-done.1), channel_id=1, source_target_pairs={{0,4},{4,8},{8,12},{12,16},{16,20},{20,24},{24,28},{28,0},{1,5},{5... | collective-permute-start | bytes 9830408 | tf_op jit(solution)/shard_map/ppermute | solution.py:17
  236.5 1.7 copy-start.5
  238.2 73.1 %collective-permute-start.3 = (bf16[256,6400]{1,0:T(8,128)(2,1)S(1)}, bf16[256,6400]{1,0:T(8,128)(2,1)S(1)}, u32[]{:S(2)}, u32[]{:S(2)}) collective-permute-start(bf16[256,6400]{1,0:T(8,128)(2,1)S(1)} %collective-permute-done.2), channel_id=1, source_target_pairs={{0,4},{4,8},{8,12},{12,16},{16,20},{20,24},{24,28},{28,0},{1,5},{5... | collective-permute-start | bytes 9830408 | tf_op jit(solution)/shard_map/ppermute | solution.py:17
  311.3 1.7 copy-start.7
  313.0 72.2 %collective-permute-start.4 = (bf16[256,6400]{1,0:T(8,128)(2,1)S(1)}, bf16[256,6400]{1,0:T(8,128)(2,1)S(1)}, u32[]{:S(2)}, u32[]{:S(2)}) collective-permute-start(bf16[256,6400]{1,0:T(8,128)(2,1)S(1)} %collective-permute-done.3), channel_id=1, source_target_pairs={{0,4},{4,8},{8,12},{12,16},{16,20},{20,24},{24,28},{28,0},{1,5},{5... | collective-permute-start | bytes 9830408 | tf_op jit(solution)/shard_map/ppermute | solution.py:17
  385.2 1.7 copy-start.9
  386.9 71.5 %collective-permute-start.5 = (bf16[256,6400]{1,0:T(8,128)(2,1)S(1)}, bf16[256,6400]{1,0:T(8,128)(2,1)}, u32[]{:S(2)}, u32[]{:S(2)}) collective-permute-start(bf16[256,6400]{1,0:T(8,128)(2,1)S(1)} %collective-permute-done.4), channel_id=1, source_target_pairs={{0,4},{4,8},{8,12},{12,16},{16,20},{20,24},{24,28},{28,0},{1,5},{5... | collective-permute-start | bytes 9830408 | tf_op jit(solution)/shard_map/ppermute | solution.py:17
  458.4 70.8 %collective-permute-start.6 = (bf16[256,6400]{1,0:T(8,128)(2,1)}, bf16[256,6400]{1,0:T(8,128)(2,1)}, u32[]{:S(2)}, u32[]{:S(2)}) collective-permute-start(bf16[256,6400]{1,0:T(8,128)(2,1)} %collective-permute-done.5), channel_id=1, source_target_pairs={{0,4},{4,8},{8,12},{12,16},{16,20},{20,24},{24,28},{28,0},{1,5},{5... | collective-permute-start | bytes 9830408 | tf_op jit(solution)/shard_map/ppermute | solution.py:17
  461.7 105.9 %copy-start.10 = (bf16[256,6400]{1,0:T(8,128)(2,1)S(1)}, bf16[256,6400]{1,0:T(8,128)(2,1)}, u32[]{:S(2)}) copy-start(bf16[256,6400]{1,0:T(8,128)(2,1)} %copy-done.9) | copy-start | bytes 9830404
  461.8 107.7 %copy-start.8 = (bf16[256,6400]{1,0:T(8,128)(2,1)S(1)}, bf16[256,6400]{1,0:T(8,128)(2,1)}, u32[]{:S(2)}) copy-start(bf16[256,6400]{1,0:T(8,128)(2,1)} %copy-done.7) | copy-start | bytes 9830404
  461.8 109.7 %copy-start.6 = (bf16[256,6400]{1,0:T(8,128)(2,1)S(1)}, bf16[256,6400]{1,0:T(8,128)(2,1)}, u32[]{:S(2)}) copy-start(bf16[256,6400]{1,0:T(8,128)(2,1)} %copy-done.5) | copy-start | bytes 9830404
  461.8 111.6 %copy-start.4 = (bf16[256,6400]{1,0:T(8,128)(2,1)S(1)}, bf16[256,6400]{1,0:T(8,128)(2,1)}, u32[]{:S(2)}) copy-start(bf16[256,6400]{1,0:T(8,128)(2,1)} %copy-done.3) | copy-start | bytes 9830404
  461.8 113.5 %copy-start.2 = (bf16[256,6400]{1,0:T(8,128)(2,1)S(1)}, bf16[256,6400]{1,0:T(8,128)(2,1)}, u32[]{:S(2)}) copy-start(bf16[256,6400]{1,0:T(8,128)(2,1)} %copy-done.1) | copy-start | bytes 9830404
  579.0 53.4 %copy-start.11 = (s32[512]{0:T(512)S(1)}, s32[512]{0:T(512)}, u32[]{:S(2)}) copy-start(s32[512]{0:T(512)} %param.7) | copy-start | bytes 6148
  579.0 87.2 %copy-start.14 = (s32[8]{0:T(128)S(1)}, s32[8]{0:T(128)}, u32[]{:S(2)}) copy-start(s32[8]{0:T(128)} %param.9) | copy-start | bytes 100
  638.2 28.7 %copy-start.12 = (f32[512]{0:T(512)}, f32[512]{0:T(512)S(1)}, u32[]{:S(2)}) copy-start(f32[512]{0:T(512)S(1)} %add_subtract_fusion) | copy-start | bytes 6148
  638.3 28.6 %copy-start.13 = (f32[25]{0:T(128)}, f32[25]{0:T(128)S(1)}, u32[]{:S(2)}) copy-start(f32[25]{0:T(128)S(1)} %fusion.2) | copy-start | bytes 304
Sparse Core Ops, SparseCore 0:
  458.5 23.0 all-gather.3
